TPU v7x, 256 devices: a whole 4x4x8 slice. The times are simulated.
256 devices in a mesh: row: 16 (over x, z_hi, core), col: 16 (over z_lo, y).
Axes of the slice: x: 4, y: 4, z: 8 (z_hi: 2, z_lo: 4; z = z_hi * 4 + z_lo), core: 2. Of those that a mesh axis runs over, the one named last changes fastest.
Arguments:
- rhs_c: float32 [3, 2048, 3, 2048], P(None, 'row', None, 'col'), may hold values from -6 to 6
- rhs_f: float32 [3, 2048, 3, 2048], P(None, 'row', None, 'col'), may hold values from -6 to 6
- pencil_a: bfloat16 [3, 2048, 3, 2048], P(None, 'row', None, 'col'), may hold values from -0.5 to 0.5
- pencil_d: bfloat16 [3, 2048, 3, 2048], P(None, 'row', None, 'col'), may hold values from -0.5 to 0.5
- pencil_b: bfloat16 [3, 2048, 3, 2048], P(None, 'row', None, 'col'), may hold values from -0.5 to 0.5
- pencil_e: bfloat16 [3, 2048, 3, 2048], P(None, 'row', None, 'col'), may hold values from -0.5 to 0.5
- d_inverse: float32 [3, 2048, 128], P(None, 'row'), may hold values from -0.25 to 2.5
- left_vectors: float32 [3, 2048, 128], P(None, 'row'), may hold values from -0.25 to 2.5
- left_inverse: float32 [3, 2048, 128], P(None, 'row'), may hold values from -0.25 to 2.5
- left_eigs: float32 [3, 2048], P(None, 'row'), may hold values from 1 to 3
- e_inverse: float32 [3, 2048, 128], P(None, 'col'), may hold values from -0.25 to 2.5
- right_vectors: float32 [3, 2048, 128], P(None, 'col'), may hold values from -0.25 to 2.5
- right_inverse: float32 [3, 2048, 128], P(None, 'col'), may hold values from -0.25 to 2.5
- right_eigs: float32 [3, 2048], P(None, 'col'), may hold values from -3 to -1
Outputs:
- updated_c: float32 [3, 2048, 3, 2048], P(None, 'row', None, 'col')
- updated_f: float32 [3, 2048, 3, 2048], P(None, 'row', None, 'col')
- solved_r: float32 [3, 2048, 3, 2048], P(None, 'row', None, 'col')
- solved_l: float32 [3, 2048, 3, 2048], P(None, 'row', None, 'col')
All inputs are finite; a program needn't handle non-finite values.
Results may differ from a plain program's by a relative error of at most 0.0003.
Values may be sent and summed in bfloat16 or wider, within the bound.
No kernel may reach another device: no remote copies, remote signals or barrier semaphores. Data moves between devices by JAX's collectives and lax.ppermute only.
A program may use at most 64 MiB of HBM per device.

v0:
```python
import jax
import jax.numpy as jnp
from jax import lax
from jax.sharding import PartitionSpec as P

TILE = 128
ORDER = 6144
STEPS = 3


def padded(value, sides, width):
    for axis, dim in sides:
        devices, length = (lax.axis_size(axis), value.shape[dim])
        up = [(i, (i + 1) % devices) for i in range(devices)]
        down = [(j, i) for i, j in up]
        last = lax.slice_in_dim(value, length - width, length, axis=dim)
        initial = lax.slice_in_dim(value, 0, width, axis=dim)
        before = lax.ppermute(last, axis, up)
        after = lax.ppermute(initial, axis, down)
        value = jnp.concatenate([before, value, after], axis=dim)
    return value


def total_of_pieces(value, axis):
    parts = lax.all_gather(value, axis)
    return parts.sum(axis=0)


def cut_along(value, dim, devices):
    before, after = (value.shape[:dim], value.shape[dim + 1 :])
    return jnp.moveaxis(value.reshape(*before, devices, -1, *after), dim, 0)


def sum_at_owner(value, axis, dim):
    devices = lax.axis_size(axis)
    parts = lax.all_to_all(cut_along(value, dim, devices), axis, 0, 0, tiled=True)
    return jnp.sum(parts, axis=0)


def filled_up(lines, devices):
    spare = -lines.shape[0] % devices
    if not spare:
        return lines
    return jnp.concatenate([lines, jnp.zeros((spare, *lines.shape[1:]), lines.dtype)])


def in_order(parts, dim):
    dims = list(parts.shape[1:])
    dims[dim] *= parts.shape[0]
    return jnp.moveaxis(parts, 0, dim).reshape(dims)


def copy_for_each(value, axis):
    copies = jnp.broadcast_to(value, (lax.axis_size(axis), *value.shape))
    return lax.all_to_all(copies, axis, split_axis=0, concat_axis=0, tiled=True)


def collect(value, axis, dim):
    return in_order(copy_for_each(value, axis), dim)


def sum_by_parts(value, axes):
    lines = value.reshape(-1, value.shape[-1])
    own = sum_at_owner(filled_up(lines, lax.axis_size(axes)), axes, 0)
    whole = collect(own, axes, 0)
    return whole[: len(lines)].reshape(value.shape)


def product(left, right):
    return jnp.einsum("bij,bjk->bik", left, right, precision=lax.Precision.HIGHEST)


def solve_tiles(
    a_diag,
    e_diag,
    resid_c,
    resid_f,
    inv_d,
    vec_left,
    back_left,
    eig_left,
    inv_e,
    vec_right,
    back_right,
    eig_right,
):
    coupled = product(a_diag, inv_d)
    merged = product(resid_c - product(coupled, resid_f), inv_e)
    spectral = product(product(back_left, merged), vec_right)
    spectral = spectral / (eig_left[:, :, None] - eig_right[:, None, :])
    new_l = product(product(vec_left, spectral), back_right)
    new_r = product(inv_d, resid_f + product(new_l, e_diag))
    return (new_r, new_l)


def body(
    rhs_c,
    rhs_f,
    pencil_a,
    pencil_d,
    pencil_b,
    pencil_e,
    d_inverse,
    left_vectors,
    left_inverse,
    left_eigs,
    e_inverse,
    right_vectors,
    right_inverse,
    right_eigs,
):
    highest = lax.Precision.HIGHEST
    count_rows = lax.axis_size("row")
    count_cols = lax.axis_size("col")
    this_row = lax.axis_index("row")
    this_col = lax.axis_index("col")
    rows_dev = rhs_c.shape[0]
    cols_dev = rhs_c.shape[2]
    blocks = ORDER // TILE
    local_rows = jnp.arange(rows_dev, dtype=jnp.int32)
    local_cols = jnp.arange(cols_dev, dtype=jnp.int32)
    block_rows = local_rows * count_rows + this_row
    block_cols = local_cols * count_cols + this_col
    near_ad = padded(jnp.stack([pencil_a, pencil_d]), (("col", 4),), TILE)
    near_ad = near_ad.reshape(2, rows_dev, TILE, cols_dev, 3, TILE)
    near_be = padded(jnp.stack([pencil_b, pencil_e]), (("row", 2),), TILE)
    near_be = near_be.reshape(2, rows_dev, 3, TILE, cols_dev, TILE)
    current_c = rhs_c
    current_f = rhs_f
    out_r = jnp.zeros_like(rhs_c)
    out_l = jnp.zeros_like(rhs_c)
    for step in range(STEPS):
        offset = 1 - step
        front_rows = block_cols + offset
        col_valid = (front_rows >= 0) & (front_rows < blocks)
        rows_clip = jnp.clip(front_rows, 0, blocks - 1)
        front_cols = block_rows - offset
        row_valid = (front_cols >= 0) & (front_cols < blocks)
        cols_clip = jnp.clip(front_cols, 0, blocks - 1)
        slot_cols = jnp.clip(rows_clip // count_cols, 0, cols_dev - 1)
        picked_ad = jnp.take(near_ad[:, :, :, :, 1 + offset, :], slot_cols, axis=3)
        panel_a = picked_ad[0]
        panel_d = picked_ad[1]
        slot_rows = jnp.clip(cols_clip // count_rows, 0, rows_dev - 1)
        picked_be = jnp.take(near_be[:, :, 1 - offset, :, :, :], slot_rows, axis=1)
        panel_b = picked_be[0]
        panel_e = picked_be[1]
        owned = col_valid & (rows_clip % count_rows == this_row)
        own_slot = jnp.clip(rows_clip // count_rows, 0, rows_dev - 1)
        resid_c = current_c[own_slot, :, local_cols, :]
        resid_f = current_f[own_slot, :, local_cols, :]
        a_diag = panel_a[own_slot, :, local_cols, :].astype(jnp.float32)
        e_diag = panel_e[own_slot, :, local_cols, :].astype(jnp.float32)
        new_r, new_l = solve_tiles(
            a_diag,
            e_diag,
            resid_c,
            resid_f,
            d_inverse[own_slot],
            left_vectors[own_slot],
            left_inverse[own_slot],
            left_eigs[own_slot],
            e_inverse,
            right_vectors,
            right_inverse,
            right_eigs,
        )
        new_r = jnp.where(owned[:, None, None], new_r, 0.0)
        new_l = jnp.where(owned[:, None, None], new_l, 0.0)
        l_slot = jnp.clip(cols_clip // count_cols, 0, cols_dev - 1)
        front_r = total_of_pieces(new_r, "row")
        picked = jnp.where((cols_clip % count_cols == this_col)[:, None, None], new_l[l_slot], 0.0)
        front_l = sum_by_parts(picked, "col")
        front_r = jnp.where(col_valid[:, None, None], front_r, 0.0)
        front_l = jnp.where(row_valid[:, None, None], front_l, 0.0)
        mask_a = (block_rows[:, None] < front_rows[None, :]) & col_valid[None, :]
        term_c = jnp.einsum(
            "apbq,bqs->apbs", panel_a.astype(jnp.float32), front_r, precision=highest
        )
        term_f = jnp.einsum(
            "apbq,bqs->apbs", panel_d.astype(jnp.float32), front_r, precision=highest
        )
        mask_b = (block_cols[None, :] > front_cols[:, None]) & row_valid[:, None]
        gain_c = jnp.einsum(
            "apq,aqbs->apbs", front_l, panel_b.astype(jnp.float32), precision=highest
        )
        gain_f = jnp.einsum(
            "apq,aqbs->apbs", front_l, panel_e.astype(jnp.float32), precision=highest
        )
        wide_a = mask_a[:, None, :, None]
        wide_b = mask_b[:, None, :, None]
        current_c = current_c - jnp.where(wide_a, term_c, 0.0) + jnp.where(wide_b, gain_c, 0.0)
        current_f = current_f - jnp.where(wide_a, term_f, 0.0) + jnp.where(wide_b, gain_f, 0.0)
        place = (owned[None, :] & (local_rows[:, None] == own_slot[None, :]))[:, None, :, None]
        out_r = out_r + jnp.where(place, new_r.transpose(1, 0, 2)[None], 0.0)
        out_l = out_l + jnp.where(place, new_l.transpose(1, 0, 2)[None], 0.0)
    return (current_c, current_f, out_r, out_l)


def solution(mesh):
    in_specs = (
        P(None, "row", None, "col"),
        P(None, "row", None, "col"),
        P(None, "row", None, "col"),
        P(None, "row", None, "col"),
        P(None, "row", None, "col"),
        P(None, "row", None, "col"),
        P(None, "row", None),
        P(None, "row", None),
        P(None, "row", None),
        P(None, "row"),
        P(None, "col", None),
        P(None, "col", None),
        P(None, "col", None),
        P(None, "col"),
    )
    out_specs = (
        P(None, "row", None, "col"),
        P(None, "row", None, "col"),
        P(None, "row", None, "col"),
        P(None, "row", None, "col"),
    )
    return jax.shard_map(body, mesh=mesh, in_specs=in_specs, out_specs=out_specs, check_vma=False)
```

profile of v0, /device:TPU:1, one launch (start us, length us, event | category | flops | bytes accessed | tf_op | source)
XLA Modules:
  0.0 337.5 jit_solution(10680067089794043893)
XLA Ops:
  7.3 1.3 copy.129
  10.6 2.1 collective-permute-start
  12.8 5.5 %collective-permute-start.1 = (bf16[2,3,128,3,128]{2,4,3,1,0:T(8,128)(2,1)}, bf16[2,3,128,3,128]{2,4,3,1,0:T(8,128)(2,1)S(1)}, u32[]{:S(2)}, u32[]{:S(2)}) collective-permute-start(bf16[2,3,128,3,128]{2,4,3,1,0:T(8,128)(2,1)} %pad_maximum_fusion.2), channel_id=1, source_target_pairs={{1,0},{2,1},{3,2},{4,3},{5,4},{6,5},{7,6},{8,7},{9,8},{10,9},{11,1... | collective-permute-start | bytes 1769480 | tf_op jit(solution)/shard_map/ppermute | solution.py:19
  18.3 1.9 pad_maximum_fusion.3
  20.2 6.6 %collective-permute-start.2 = (bf16[2,3,128,3,128]{4,2,3,1,0:T(8,128)(2,1)}, bf16[2,3,128,3,128]{4,2,3,1,0:T(8,128)(2,1)S(1)}, u32[]{:S(2)}, u32[]{:S(2)}) collective-permute-start(bf16[2,3,128,3,128]{4,2,3,1,0:T(8,128)(2,1)} %pad_maximum_fusion.3), channel_id=1, source_target_pairs={{0,16},{16,32},{32,48},{48,64},{64,80},{80,96},{96,112},{112,128},... | collective-permute-start | bytes 1769480 | tf_op jit(solution)/shard_map/ppermute | solution.py:18
  26.8 2.3 gather_fusion.1
  29.2 2.3 gather_fusion.4
  31.5 1.2 gather_fusion
  35.1 1.2 gather_fusion.2
  42.9 20.1 %collective-permute-done.3 = bf16[2,3,128,3,128]{4,2,3,1,0:T(8,128)(2,1)} collective-permute-done((bf16[2,3,128,3,128]{4,2,3,1,0:T(8,128)(2,1)}, bf16[2,3,128,3,128]{4,2,3,1,0:T(8,128)(2,1)}, u32[]{:S(2)}, u32[]{:S(2)}) %collective-permute-start.3) | collective-permute-done | bytes 589856 | tf_op jit(solution)/shard_map/ppermute | solution.py:19
  67.2 1.3 fusion.110
  68.5 1.4 convolution_subtract_fusion.2
  69.8 1.3 fusion.111
  71.1 1.3 fusion.112
  72.4 1.3 convolution_divide_fusion.2
  74.5 1.2 convolution_add_fusion.2
  76.8 2.1 copy.139
  78.9 2.1 copy.136
  81.1 1.2 gather_fusion.9
  82.3 1.3 gather_fusion.12
  84.6 1.2 gather_fusion.11
  91.2 4.2 %all-to-all-start = ((f32[16,24,128]{2,1,0:T(8,128)}), f32[16,24,128]{2,1,0:T(8,128)}, u32[]{:S(2)}, u32[]{:S(2)}) async-start(f32[16,24,128]{2,1,0:T(8,128)} %broadcast_select_fusion.2), calls=%async_computation | async-start | bytes 393216 | tf_op jit(solution)/shard_map/all_to_all | solution.py:36
  99.5 2.2 gather_fusion.14
  105.3 5.9 %all-to-all-start.1 = ((f32[16,24,128]{2,1,0:T(8,128)}), f32[16,24,128]{2,1,0:T(8,128)}, u32[]{:S(2)}, u32[]{:S(2)}) async-start(f32[16,24,128]{2,1,0:T(8,128)} %broadcast_in_dim.377), calls=%async_computation.1 | async-start | bytes 393216 | tf_op jit(solution)/shard_map/all_to_all | solution.py:55
  111.4 1.9 fusion.114
  113.3 2.2 gather_fusion.16
  115.5 20.8 %all-gather.7.cloned.1.call-done = f32[48,128,128]{2,1,0:T(8,128)} async-done(((f32[3,128,128]{2,1,0:T(8,128)}), f32[48,128,128]{2,1,0:T(8,128)}) %all-gather.7.cloned.1.call-update) | async-done | bytes 3145744 | tf_op jit(solution)/shard_map/all_gather | solution.py:25
  136.3 2.8 reduce_sum.54
  139.1 2.3 fusion.14
  141.4 1.7 fusion.12
  143.2 1.2 gather_fusion.10
  144.4 1.5 fusion.17
  145.9 1.6 fusion.15
  148.1 1.6 convolution_subtract_fusion.1
  149.7 1.5 fusion.115
  151.2 1.3 fusion.116
  152.5 1.3 convolution_divide_fusion.1
  153.7 1.3 fusion.117
  155.0 1.7 broadcast_select_fusion.4
  156.7 1.3 convolution_add_fusion.1
  158.1 2.1 convolution_select_fusion.7
  160.3 1.2 gather_fusion.18
  163.9 2.2 gather_fusion.20
  173.5 13.0 %all-to-all-start.2 = ((f32[16,24,128]{2,1,0:T(8,128)}), f32[16,24,128]{2,1,0:T(8,128)S(1)}, u32[]{:S(2)}, u32[]{:S(2)}) async-start(f32[16,24,128]{2,1,0:T(8,128)} %broadcast_select_fusion.1), calls=%async_computation.2 | async-start | bytes 393216 | tf_op jit(solution)/shard_map/all_to_all | solution.py:36
  188.6 1.9 fusion.118
  190.4 5.0 %all-to-all-done.2 = f32[16,24,128]{2,1,0:T(8,128)S(1)} async-done(((f32[16,24,128]{2,1,0:T(8,128)}), f32[16,24,128]{2,1,0:T(8,128)S(1)}, u32[]{:S(2)}, u32[]{:S(2)}) %all-to-all-start.2) | async-done | bytes 196640 | tf_op jit(solution)/shard_map/all_to_all | solution.py:36
  196.2 4.2 %all-to-all-start.3 = ((f32[16,24,128]{2,1,0:T(8,128)}), f32[16,24,128]{2,1,0:T(8,128)}, u32[]{:S(2)}, u32[]{:S(2)}) async-start(f32[16,24,128]{2,1,0:T(8,128)} %broadcast_in_dim.386), calls=%async_computation.3 | async-start | bytes 393216 | tf_op jit(solution)/shard_map/all_to_all | solution.py:55
  200.7 28.7 %all-gather.9.cloned.1.call-done = f32[48,128,128]{2,1,0:T(8,128)} async-done(((f32[3,128,128]{2,1,0:T(8,128)}), f32[48,128,128]{2,1,0:T(8,128)}) %all-gather.9.cloned.1.call-update) | async-done | bytes 3145744 | tf_op jit(solution)/shard_map/all_gather | solution.py:25
  229.4 2.1 reduce_sum.56
  233.4 1.5 fusion.11
  235.0 1.5 fusion.6
  237.1 1.6 fusion.9
  239.3 1.5 convolution_subtract_fusion
  241.3 1.3 fusion.120
  242.6 1.3 convolution_divide_fusion
  245.3 1.3 convolution_add_fusion
  246.6 1.9 convolution_select_fusion.6
  251.4 10.6 %all-to-all-start.4 = ((f32[16,24,128]{2,1,0:T(8,128)}), f32[16,24,128]{2,1,0:T(8,128)}, u32[]{:S(2)}, u32[]{:S(2)}) async-start(f32[16,24,128]{2,1,0:T(8,128)} %broadcast_select_fusion), calls=%async_computation.4 | async-start | bytes 393216 | tf_op jit(solution)/shard_map/all_to_all | solution.py:36
  267.2 1.5 select_add_fusion
  272.7 7.7 %all-to-all-start.5 = ((f32[16,24,128]{2,1,0:T(8,128)}), f32[16,24,128]{2,1,0:T(8,128)S(1)}, u32[]{:S(2)}, u32[]{:S(2)}) async-start(f32[16,24,128]{2,1,0:T(8,128)} %broadcast_in_dim.395), calls=%async_computation.5 | async-start | bytes 393216 | tf_op jit(solution)/shard_map/all_to_all | solution.py:55
  280.4 42.2 %all-gather.11.cloned.1.call-done = f32[48,128,128]{2,1,0:T(8,128)} async-done(((f32[3,128,128]{2,1,0:T(8,128)}), f32[48,128,128]{2,1,0:T(8,128)}) %all-gather.11.cloned.1.call-update) | async-done | bytes 3145744 | tf_op jit(solution)/shard_map/all_gather | solution.py:25
  322.6 2.1 reduce_sum.58
  325.9 1.5 fusion
  328.4 1.5 fusion.3
  (224 shorter events, 64.7 us)
Async XLA Ops:
  7.2 66.9 %copy-start = (f32[3,128,128]{2,1,0:T(8,128)S(1)}, f32[3,128,128]{2,1,0:T(8,128)}, u32[]{:S(2)}) copy-start(f32[3,128,128]{2,1,0:T(8,128)} %param.30) | copy-start | bytes 589828
  7.2 24.3 %copy-start.7 = (f32[3,128,128]{2,1,0:T(8,128)S(1)}, f32[3,128,128]{2,1,0:T(8,128)}, u32[]{:S(2)}) copy-start(f32[3,128,128]{2,1,0:T(8,128)} %param.24) | copy-start | bytes 589828
  7.2 25.5 %copy-start.8 = (f32[3,128,128]{2,1,0:T(8,128)S(1)}, f32[3,128,128]{2,1,0:T(8,128)}, u32[]{:S(2)}) copy-start(f32[3,128,128]{2,1,0:T(8,128)} %param.26) | copy-start | bytes 589828
  7.2 26.8 %copy-start.25 = (f32[3,128]{1,0:T(4,128)S(1)}, f32[3,128]{1,0:T(4,128)}, u32[]{:S(2)}) copy-start(f32[3,128]{1,0:T(4,128)} %param.27) | copy-start | bytes 4612
  7.2 27.9 %copy-start.9 = (f32[3,128,128]{2,1,0:T(8,128)S(1)}, f32[3,128,128]{2,1,0:T(8,128)}, u32[]{:S(2)}) copy-start(f32[3,128,128]{2,1,0:T(8,128)} %param.25) | copy-start | bytes 589828
  7.2 129.1 %all-gather.7.cloned.1.call-start = ((), (), s32[]{:S(2)}) async-start(), calls=%async_computation.6 | async-start | bytes 3342336 | tf_op jit(solution)/shard_map/all_gather | solution.py:25
  10.6 26.9 %collective-permute-start = (bf16[2,3,128,3,128]{2,4,3,1,0:T(8,128)(2,1)}, bf16[2,3,128,3,128]{2,4,3,1,0:T(8,128)(2,1)S(1)}, u32[]{:S(2)}, u32[]{:S(2)}) collective-permute-start(bf16[2,3,128,3,128]{2,4,3,1,0:T(8,128)(2,1)} %pad_maximum_fusion.2), channel_id=1, source_target_pairs={{0,1},{1,2},{2,3},{3,4},{4,5},{5,6},{6,7},{7,8},{8,9},{9,10},{10,1... | collective-permute-start | bytes 1769480 | tf_op jit(solution)/shard_map/ppermute | solution.py:18
  12.8 24.8 %collective-permute-start.1 = (bf16[2,3,128,3,128]{2,4,3,1,0:T(8,128)(2,1)}, bf16[2,3,128,3,128]{2,4,3,1,0:T(8,128)(2,1)S(1)}, u32[]{:S(2)}, u32[]{:S(2)}) collective-permute-start(bf16[2,3,128,3,128]{2,4,3,1,0:T(8,128)(2,1)} %pad_maximum_fusion.2), channel_id=1, source_target_pairs={{1,0},{2,1},{3,2},{4,3},{5,4},{6,5},{7,6},{8,7},{9,8},{10,9},{11,1... | collective-permute-start | bytes 1769480 | tf_op jit(solution)/shard_map/ppermute | solution.py:19
  20.2 22.7 %collective-permute-start.2 = (bf16[2,3,128,3,128]{4,2,3,1,0:T(8,128)(2,1)}, bf16[2,3,128,3,128]{4,2,3,1,0:T(8,128)(2,1)S(1)}, u32[]{:S(2)}, u32[]{:S(2)}) collective-permute-start(bf16[2,3,128,3,128]{4,2,3,1,0:T(8,128)(2,1)} %pad_maximum_fusion.3), channel_id=1, source_target_pairs={{0,16},{16,32},{32,48},{48,64},{64,80},{80,96},{96,112},{112,128},... | collective-permute-start | bytes 1769480 | tf_op jit(solution)/shard_map/ppermute | solution.py:18
  26.8 36.2 %collective-permute-start.3 = (bf16[2,3,128,3,128]{4,2,3,1,0:T(8,128)(2,1)}, bf16[2,3,128,3,128]{4,2,3,1,0:T(8,128)(2,1)}, u32[]{:S(2)}, u32[]{:S(2)}) collective-permute-start(bf16[2,3,128,3,128]{4,2,3,1,0:T(8,128)(2,1)} %pad_maximum_fusion.3), channel_id=1, source_target_pairs={{16,0},{32,16},{48,32},{64,48},{80,64},{96,80},{112,96},{128,112},... | collective-permute-start | bytes 1769480 | tf_op jit(solution)/shard_map/ppermute | solution.py:19
  38.8 24.1 %copy-start.23 = (bf16[3,128,3,128]{3,1,2,0:T(8,128)(2,1)S(1)}, bf16[3,128,3,128]{3,1,2,0:T(8,128)(2,1)}, u32[]{:S(2)}) copy-start(bf16[3,128,3,128]{3,1,2,0:T(8,128)(2,1)} %param.23) | copy-start | bytes 884740
  38.8 24.1 %copy-start.24 = (bf16[3,128,3,128]{3,1,2,0:T(8,128)(2,1)S(1)}, bf16[3,128,3,128]{3,1,2,0:T(8,128)(2,1)}, u32[]{:S(2)}) copy-start(bf16[3,128,3,128]{3,1,2,0:T(8,128)(2,1)} %param.22) | copy-start | bytes 884740
  64.2 0.9 copy-start.41
  65.1 9.0 %copy-start.37 = (pred[3]{0:T(512)(128)(4,1)S(1)}, pred[3]{0:T(512)(128)(4,1)}, u32[]{:S(2)}) copy-start(pred[3]{0:T(512)(128)(4,1)} %get-tuple-element.55) | copy-start | bytes 13
  65.2 8.5 %copy-start.27 = (f32[3,128,128]{2,1,0:T(8,128)S(1)}, f32[3,128,128]{2,1,0:T(8,128)}, u32[]{:S(2)}) copy-start(f32[3,128,128]{2,1,0:T(8,128)} %gather_fusion.2) | copy-start | bytes 589828
  66.0 8.5 %copy-start.22 = (bf16[3,128,3,128]{3,1,2,0:T(8,128)(2,1)}, bf16[3,128,3,128]{3,1,2,0:T(8,128)(2,1)S(1)}, u32[]{:S(2)}) copy-start(bf16[3,128,3,128]{3,1,2,0:T(8,128)(2,1)S(1)} %get-tuple-element.33) | copy-start | bytes 884740
  66.0 9.7 %copy-start.19 = (f32[3,128,128]{2,1,0:T(8,128)S(1)}, f32[3,128,128]{2,1,0:T(8,128)}, u32[]{:S(2)}) copy-start(f32[3,128,128]{2,1,0:T(8,128)} %gather_fusion) | copy-start | bytes 589828
  67.2 7.3 %copy-start.28 = (bf16[3,128,128]{2,1,0:T(8,128)(2,1)S(1)}, bf16[3,128,128]{2,1,0:T(8,128)(2,1)}, u32[]{:S(2)}) copy-start(bf16[3,128,128]{2,1,0:T(8,128)(2,1)} %gather_fusion.7) | copy-start | bytes 294916
  73.7 11.0 %copy-start.10 = (f32[3,128,128]{2,1,0:T(8,128)S(1)}, f32[3,128,128]{2,1,0:T(8,128)}, u32[]{:S(2)}) copy-start(f32[3,128,128]{2,1,0:T(8,128)} %param.25) | copy-start | bytes 589828
  74.4 16.7 %copy-start.11 = (f32[3,128,128]{2,1,0:T(8,128)}, f32[3,128,128]{2,1,0:T(8,128)S(1)}, u32[]{:S(2)}) copy-start(f32[3,128,128]{2,1,0:T(8,128)S(1)} %get-tuple-element.42) | copy-start | bytes 589828
  74.5 20.9 %copy-start.4 = (bf16[2,3,128,3,1,128]{2,5,4,3,1,0:T(8,128)(2,1)S(1)}, bf16[2,3,128,3,1,128]{2,5,4,3,1,0:T(8,128)(2,1)}, u32[]{:S(2)}) copy-start(bf16[2,3,128,3,1,128]{2,5,4,3,1,0:T(8,128)(2,1)} %get-tuple-element.26) | copy-start | bytes 1769476
  86.7 8.6 %copy-start.29 = (pred[3]{0:T(512)(128)(4,1)}, pred[3]{0:T(512)(128)(4,1)S(1)}, u32[]{:S(2)}) copy-start(pred[3]{0:T(512)(128)(4,1)S(1)} %get-tuple-element.72) | copy-start | bytes 13
  86.7 8.6 %copy-start.30 = (pred[3]{0:T(512)(128)(4,1)}, pred[3]{0:T(512)(128)(4,1)S(1)}, u32[]{:S(2)}) copy-start(pred[3]{0:T(512)(128)(4,1)S(1)} %get-tuple-element.73) | copy-start | bytes 13
  87.3 8.1 %copy-start.35 = (pred[3]{0:T(512)(128)(4,1)}, pred[3]{0:T(512)(128)(4,1)S(1)}, u32[]{:S(2)}) copy-start(pred[3]{0:T(512)(128)(4,1)S(1)} %get-tuple-element.63) | copy-start | bytes 13
  87.9 7.5 %copy-start.31 = (pred[3]{0:T(512)(128)(4,1)}, pred[3]{0:T(512)(128)(4,1)S(1)}, u32[]{:S(2)}) copy-start(pred[3]{0:T(512)(128)(4,1)S(1)} %get-tuple-element.53) | copy-start | bytes 13
  91.2 12.5 %all-to-all-start = ((f32[16,24,128]{2,1,0:T(8,128)}), f32[16,24,128]{2,1,0:T(8,128)}, u32[]{:S(2)}, u32[]{:S(2)}) async-start(f32[16,24,128]{2,1,0:T(8,128)} %broadcast_select_fusion.2), calls=%async_computation | async-start | bytes 393216 | tf_op jit(solution)/shard_map/all_to_all | solution.py:36
  99.5 39.6 %copy-start.6 = (f32[3,128,3,128]{1,3,0,2:T(8,128)S(1)}, f32[3,128,3,128]{1,3,0,2:T(8,128)}, u32[]{:S(2)}) copy-start(f32[3,128,3,128]{1,3,0,2:T(8,128)} %copy.139) | copy-start | bytes 1769476
  105.3 36.1 %all-to-all-start.1 = ((f32[16,24,128]{2,1,0:T(8,128)}), f32[16,24,128]{2,1,0:T(8,128)}, u32[]{:S(2)}, u32[]{:S(2)}) async-start(f32[16,24,128]{2,1,0:T(8,128)} %broadcast_in_dim.377), calls=%async_computation.1 | async-start | bytes 393216 | tf_op jit(solution)/shard_map/all_to_all | solution.py:55
  111.2 118.2 %all-gather.9.cloned.1.call-start = ((), (), s32[]{:S(2)}) async-start(), calls=%async_computation.7 | async-start | bytes 3342336 | tf_op jit(solution)/shard_map/all_gather | solution.py:25
  136.3 8.1 %copy-start.5 = (f32[3,128,3,128]{1,3,0,2:T(8,128)S(1)}, f32[3,128,3,128]{1,3,0,2:T(8,128)}, u32[]{:S(2)}) copy-start(f32[3,128,3,128]{1,3,0,2:T(8,128)} %copy.136) | copy-start | bytes 1769476
  147.5 14.0 %copy-start.1 = (f32[3,128,3,128]{1,3,0,2:T(8,128)}, f32[3,128,3,128]{1,3,0,2:T(8,128)S(1)}, u32[]{:S(2)}) copy-start(f32[3,128,3,128]{1,3,0,2:T(8,128)S(1)} %fusion.15) | copy-start | bytes 1769476
  149.7 18.4 %copy-start.3 = (bf16[2,3,128,3,1,128]{2,5,4,3,1,0:T(8,128)(2,1)S(1)}, bf16[2,3,128,3,1,128]{2,5,4,3,1,0:T(8,128)(2,1)}, u32[]{:S(2)}) copy-start(bf16[2,3,128,3,1,128]{2,5,4,3,1,0:T(8,128)(2,1)} %get-tuple-element.25) | copy-start | bytes 1769476
  168.4 3.6 %copy-start.14 = (f32[3,128,128]{2,1,0:T(8,128)S(1)}, f32[3,128,128]{2,1,0:T(8,128)}, u32[]{:S(2)}) copy-start(f32[3,128,128]{2,1,0:T(8,128)} %get-tuple-element.44) | copy-start | bytes 589828
  169.3 19.3 %copy-start.17 = (f32[3,128,128]{2,1,0:T(8,128)S(1)}, f32[3,128,128]{2,1,0:T(8,128)}, u32[]{:S(2)}) copy-start(f32[3,128,128]{2,1,0:T(8,128)} %gather_fusion.18) | copy-start | bytes 589828
  173.5 58.6 %copy-start.36 = (pred[3]{0:T(512)(128)(4,1)S(1)}, pred[3]{0:T(512)(128)(4,1)}, u32[]{:S(2)}) copy-start(pred[3]{0:T(512)(128)(4,1)} %copy-done.35) | copy-start | bytes 13
  173.5 22.0 %all-to-all-start.2 = ((f32[16,24,128]{2,1,0:T(8,128)}), f32[16,24,128]{2,1,0:T(8,128)S(1)}, u32[]{:S(2)}, u32[]{:S(2)}) async-start(f32[16,24,128]{2,1,0:T(8,128)} %broadcast_select_fusion.1), calls=%async_computation.2 | async-start | bytes 393216 | tf_op jit(solution)/shard_map/all_to_all | solution.py:36
  187.3 44.1 %copy-start.21 = (bf16[3,128,3,128]{3,1,2,0:T(8,128)(2,1)}, bf16[3,128,3,128]{3,1,2,0:T(8,128)(2,1)S(1)}, u32[]{:S(2)}) copy-start(bf16[3,128,3,128]{3,1,2,0:T(8,128)(2,1)S(1)} %get-tuple-element.29) | copy-start | bytes 884740
  188.6 44.8 %copy-start.2 = (f32[3,128,3,128]{1,3,0,2:T(8,128)S(1)}, f32[3,128,3,128]{1,3,0,2:T(8,128)}, u32[]{:S(2)}) copy-start(f32[3,128,3,128]{1,3,0,2:T(8,128)} %copy-done.1) | copy-start | bytes 1769476
  196.2 38.8 %all-to-all-start.3 = ((f32[16,24,128]{2,1,0:T(8,128)}), f32[16,24,128]{2,1,0:T(8,128)}, u32[]{:S(2)}, u32[]{:S(2)}) async-start(f32[16,24,128]{2,1,0:T(8,128)} %broadcast_in_dim.386), calls=%async_computation.3 | async-start | bytes 393216 | tf_op jit(solution)/shard_map/all_to_all | solution.py:55
  200.4 122.3 %all-gather.11.cloned.1.call-start = ((), (), s32[]{:S(2)}) async-start(), calls=%async_computation.8 | async-start | bytes 3342336 | tf_op jit(solution)/shard_map/all_gather | solution.py:25
  231.5 0.7 copy-start.20
  233.4 7.4 %copy-start.16 = (f32[3,128,128]{2,1,0:T(8,128)S(1)}, f32[3,128,128]{2,1,0:T(8,128)}, u32[]{:S(2)}) copy-start(f32[3,128,128]{2,1,0:T(8,128)} %param.28) | copy-start | bytes 589828
  236.5 7.4 %copy-start.26 = (f32[3,128,128]{2,1,0:T(8,128)S(1)}, f32[3,128,128]{2,1,0:T(8,128)}, u32[]{:S(2)}) copy-start(f32[3,128,128]{2,1,0:T(8,128)} %gather_fusion.20) | copy-start | bytes 589828
  237.1 9.4 %copy-start.18 = (f32[3,128,128]{2,1,0:T(8,128)S(1)}, f32[3,128,128]{2,1,0:T(8,128)}, u32[]{:S(2)}) copy-start(f32[3,128,128]{2,1,0:T(8,128)} %gather_fusion.18) | copy-start | bytes 589828
  238.7 10.0 %copy-start.38 = (pred[3]{0:T(512)(128)(4,1)S(1)}, pred[3]{0:T(512)(128)(4,1)}, u32[]{:S(2)}) copy-start(pred[3]{0:T(512)(128)(4,1)} %get-tuple-element.55) | copy-start | bytes 13
  238.7 10.7 %copy-start.39 = (pred[3]{0:T(512)(128)(4,1)S(1)}, pred[3]{0:T(512)(128)(4,1)}, u32[]{:S(2)}) copy-start(pred[3]{0:T(512)(128)(4,1)} %get-tuple-element.57) | copy-start | bytes 13
  240.8 21.3 %copy-start.40 = (pred[3]{0:T(512)(128)(4,1)S(1)}, pred[3]{0:T(512)(128)(4,1)}, u32[]{:S(2)}) copy-start(pred[3]{0:T(512)(128)(4,1)} %get-tuple-element.51) | copy-start | bytes 13
  240.8 21.9 %copy-start.13 = (f32[3,128,128]{2,1,0:T(8,128)S(1)}, f32[3,128,128]{2,1,0:T(8,128)}, u32[]{:S(2)}) copy-start(f32[3,128,128]{2,1,0:T(8,128)} %convolution_select_fusion.8) | copy-start | bytes 589828
  240.8 22.1 %copy-start.12 = (f32[3,128,128]{2,1,0:T(8,128)S(1)}, f32[3,128,128]{2,1,0:T(8,128)}, u32[]{:S(2)}) copy-start(f32[3,128,128]{2,1,0:T(8,128)} %copy-done.11) | copy-start | bytes 589828
  241.3 22.4 %copy-start.15 = (f32[3,128,128]{2,1,0:T(8,128)S(1)}, f32[3,128,128]{2,1,0:T(8,128)}, u32[]{:S(2)}) copy-start(f32[3,128,128]{2,1,0:T(8,128)} %convolution_select_fusion.7) | copy-start | bytes 589828
  249.4 17.8 %copy-start.42 = (pred[3,3]{0,1:T(4,128)(4,1)S(1)}, pred[3,3]{0,1:T(4,128)(4,1)}, u32[]{:S(2)}) copy-start(pred[3,3]{0,1:T(4,128)(4,1)} %fusion.78) | copy-start | bytes 31
  250.0 17.2 %copy-start.43 = (pred[3,3]{0,1:T(4,128)(4,1)S(1)}, pred[3,3]{0,1:T(4,128)(4,1)}, u32[]{:S(2)}) copy-start(pred[3,3]{0,1:T(4,128)(4,1)} %fusion.79) | copy-start | bytes 31
  251.4 19.6 %all-to-all-start.4 = ((f32[16,24,128]{2,1,0:T(8,128)}), f32[16,24,128]{2,1,0:T(8,128)}, u32[]{:S(2)}, u32[]{:S(2)}) async-start(f32[16,24,128]{2,1,0:T(8,128)} %broadcast_select_fusion), calls=%async_computation.4 | async-start | bytes 393216 | tf_op jit(solution)/shard_map/all_to_all | solution.py:36
  268.7 56.0 %copy-start.34 = (pred[3,3]{0,1:T(4,128)(4,1)S(1)}, pred[3,3]{0,1:T(4,128)(4,1)}, u32[]{:S(2)}) copy-start(pred[3,3]{0,1:T(4,128)(4,1)} %get-tuple-element.39) | copy-start | bytes 31
  272.7 53.2 %all-to-all-start.5 = ((f32[16,24,128]{2,1,0:T(8,128)}), f32[16,24,128]{2,1,0:T(8,128)S(1)}, u32[]{:S(2)}, u32[]{:S(2)}) async-start(f32[16,24,128]{2,1,0:T(8,128)} %broadcast_in_dim.395), calls=%async_computation.5 | async-start | bytes 393216 | tf_op jit(solution)/shard_map/all_to_all | solution.py:55
  322.6 3.2 copy-start.32
  322.6 3.2 copy-start.33
Sparse Core Ops, SparseCore 0:
  76.9 59.3 all-gather.6
  160.3 69.0 all-gather.8
  248.6 74.0 all-gather.10
where the time goes:
time: 339 us; the launch traced here: 338 us
  waiting for transfers between devices  119 us (35%)
  local copies, waits for them, and re-layouts  62.7 us (18%)
  starting transfers between devices  60.4 us (18%)
  matrix products  51.4 us (15%)
  other arithmetic  29 us (9%)
  between operations  14.8 us (4%)
    all_gather x3, waiting for transfers between devices, total_of_pieces(): parts = lax.all_gather(value, axis)  91.7 us
    dot_general x27, matrix products, product(): jnp.einsum('bij,bjk->bik', left, right, precision=lax.Precision.HIGHEST)  34.3 us
    all_to_all x3, starting transfers between devices, sum_at_owner(): lax.all_to_all(cut_along(value, dim, devices), axis, 0, 0, tiled=True)  27.8 us
    ppermute x2, waiting for transfers between devices, padded(): after = lax.ppermute(initial, axis, down)  20.1 us
    all_to_all x3, starting transfers between devices, copy_for_each(): return lax.all_to_all(copies, axis, split_axis=0, concat_axis=0, tiled=True)  17.8 us
    unnamed x96, local copies, waits for them, and re-layouts  11.8 us
    ppermute x2, starting transfers between devices, padded(): before = lax.ppermute(last, axis, up)  8.72 us
    reduce_sum x3, other arithmetic, total_of_pieces(): return parts.sum(axis=0)  6.93 us
  transfers between devices with their start and end apart: 13, of which 8 were waited for; matrix products, arithmetic and copies ran while one was open for 26% of the time, Pallas kernels for 0%

commit v1 on v0

v1 whole, which is shorter than its diff:
```python
import functools

import jax
import jax.numpy as jnp
import numpy as np
from jax import lax
from jax.experimental import pallas as pl
from jax.experimental.pallas import tpu as pltpu
from jax.sharding import PartitionSpec as P


TILE = 128
AXES = ("row", "col")

UPPER = ((0, 0), (0, 1), (0, 2), (1, 1), (1, 2), (2, 2))
SIDE = 16


def split(value):
    high = value.astype(jnp.bfloat16)
    low = (value - high.astype(jnp.float32)).astype(jnp.bfloat16)
    return high, low


def dot(left, right):
    return jnp.dot(left, right, preferred_element_type=jnp.float32)


def mul(left, right):
    lh, ll = split(left)
    rh, rl = split(right)
    return dot(lh, rh) + (dot(lh, rl) + dot(ll, rh))


def mul_bl(left, right):
    rh, rl = split(right)
    return dot(left, rh) + dot(left, rl)


def mul_br(left, right):
    lh, ll = split(left)
    return dot(lh, right) + dot(ll, right)


def row_of(ref, index):
    return ref[pl.ds(index, 1), :]


def finish(b, a, valid, cc, ff, ux, g, ve, du, dinv, u, uinv, vinv, x, y, out_r, out_l):
    m = mul(uinv, cc) - mul(ux, ff)
    w = mul(m, g)
    w = w / (x.reshape(TILE, 1) - y)
    new_l = mul(u, mul(w, vinv))
    new_r = mul(dinv, ff) + mul(du, mul(w, ve))

    @pl.when(valid)
    def _():
        out_r[b] = new_r
        out_l[a] = new_l


def each_slot(scal, fn):
    shift = scal[1]
    for b in range(3):
        row = b + shift
        valid = (row >= 0) & (row <= 2)
        fn(b, jnp.clip(row, 0, 2), valid)


def near_kernel(scal, pa, pd, pb, pe, near_ad, near_be, a_own, e_own):
    row, col = (scal[2], scal[3])
    ahead = lax.rem(col - row + SIDE, SIDE)
    up = jnp.where(row + ahead >= SIDE, 1, 0)
    back = jnp.where(col < ahead, 1, 0)
    for i in range(3):
        right = jnp.minimum(i + up, 2)
        above = jnp.maximum(i - back, 0)
        near_ad[0, i] = pa[i, right]
        near_ad[1, i] = pd[i, right]
        near_be[0, i] = pb[above, i]
        near_be[1, i] = pe[above, i]
        a_own[i] = pa[i, i]
        e_own[i] = pe[i, i]


def upper_kernel(scal, pa, pd, pb, pe, upper_ad, upper_be):
    for at, (a, b) in enumerate(UPPER):
        upper_ad[0, at] = pa[a, b]
        upper_ad[1, at] = pd[a, b]
        upper_be[0, at] = pb[a, b]
        upper_be[1, at] = pe[a, b]


def first_kernel(
    scal, cc, ff, a_own, e_own, col_m, col_p, row_p, row_m, dinv, u, uinv, x, einv, v, vinv, y,
    ux_o, g_o, ve_o, du_o, out_r, out_l,
):
    role = scal[0]
    out_r[...] = jnp.zeros_like(out_r)
    out_l[...] = jnp.zeros_like(out_l)

    @pl.when(role < 3)
    def _():
        def prepare(b, a, valid):
            a_diag = jnp.where(role == 0, col_m[0, a], jnp.where(role == 1, a_own[a], col_p[a]))
            e_diag = jnp.where(role == 0, row_p[1, b], jnp.where(role == 1, e_own[b], row_m[b]))
            coupled = mul_bl(a_diag, dinv[a])
            ux_o[b] = mul(uinv[a], coupled)
            g_o[b] = mul(einv[b], v[b])
            ve_o[b] = mul_br(vinv[b], e_diag)
            du_o[b] = mul(dinv[a], u[a])

        each_slot(scal, prepare)

    @pl.when(role == 0)
    def _():
        def solve(b, a, valid):
            finish(
                b, a, valid, cc[a, b], ff[a, b], ux_o[b], g_o[b], ve_o[b], du_o[b],
                dinv[a], u[a], uinv[a], vinv[b], row_of(x, a), row_of(y, b), out_r, out_l,
            )

        each_slot(scal, solve)


def next_kernel(
    step, scal, cc, ff, pa, pd, pb, pe, col_m, row_p, r_old, l_old,
    dinv, u, uinv, x, vinv, y, ux, g, ve, du, out_r, out_l,
):
    role = scal[0]
    out_r[...] = jnp.zeros_like(out_r)
    out_l[...] = jnp.zeros_like(out_l)
    if step == 1:
        r_far, l_far = (r_old, l_old)
        new_r, new_l = (out_r.at[1], out_l.at[1])
    else:
        r_far, l_far, r_near, l_near = (r_old.at[0], l_old.at[0], r_old.at[1], l_old.at[1])
        new_r, new_l = (out_r, out_l)

    @pl.when(role == step)
    def _():
        if step == 1:
            out_r[0] = r_far[...]
            out_l[0] = l_far[...]

        def solve(b, a, valid):
            c_now = cc[a, b] - mul_bl(col_m[0, a], r_far[b]) + mul_br(l_far[a], row_p[0, b])
            f_now = ff[a, b] - mul_bl(col_m[1, a], r_far[b]) + mul_br(l_far[a], row_p[1, b])
            if step == 2:
                c_now += mul_br(l_near[a], pb[a, b]) - mul_bl(pa[a, b], r_near[b])
                f_now += mul_br(l_near[a], pe[a, b]) - mul_bl(pd[a, b], r_near[b])
            finish(
                b, a, valid, c_now, f_now, ux[b], g[b], ve[b], du[b],
                dinv[a], u[a], uinv[a], vinv[b], row_of(x, a), row_of(y, b), new_r, new_l,
            )

        each_slot(scal, solve)


def last_kernel(
    scal, cc, ff, pa, pd, pb, pe, ad_next, ad_prev, be_prev, be_next, fr_old, fl_old, fr, fl,
    r0, l0, r1, l1, r2, l2, c_out, f_out, r_out, l_out,
):
    role, row, col = (scal[0], scal[2], scal[3])
    diff = col - row
    c_out[...] = cc[...]
    f_out[...] = ff[...]
    r_out[...] = jnp.zeros_like(r_out)
    l_out[...] = jnp.zeros_like(l_out)
    for at, (a, b) in enumerate(UPPER):
        nxt = at + jnp.where(col == SIDE - 1, 1, 0) if b < 2 else at
        prv = at - jnp.where(col == 0, 1, 0) if b > a else at
        above = at - jnp.where(row == 0, 2 if a == 1 else 1, 0) if a > 0 else at
        below = at + jnp.where(row == SIDE - 1, 2 if a == 0 else 1, 0) if b > a else at
        tiles_c = (ad_next[0, nxt], pa[a, b], ad_prev[0, prv])
        tiles_f = (ad_next[1, nxt], pd[a, b], ad_prev[1, prv])
        lines_c = (be_prev[0, above], pb[a, b], be_next[0, below])
        lines_f = (be_prev[1, above], pe[a, b], be_next[1, below])
        sum_c = cc[a, b]
        sum_f = ff[a, b]
        for s in range(3):
            on = SIDE * (b - a) + diff >= s
            rh, rl = split(jnp.where(on, fr[b] if s == 2 else fr_old[s, b], 0.0))
            lh, ll = split(jnp.where(on, fl[a] if s == 2 else fl_old[s, a], 0.0))
            sum_c += (dot(lh, lines_c[s]) + dot(ll, lines_c[s])) - (dot(tiles_c[s], rh) + dot(tiles_c[s], rl))
            sum_f += (dot(lh, lines_f[s]) + dot(ll, lines_f[s])) - (dot(tiles_f[s], rh) + dot(tiles_f[s], rl))
        c_out[a, b] = sum_c
        f_out[a, b] = sum_f

    @pl.when(role < 3)
    def _():
        def place(b, a, valid):
            @pl.when(valid)
            def _():
                r_out[a, b] = r0[b] + r1[1, b] + r2[b]
                l_out[a, b] = l0[a] + l1[1, a] + l2[a]

        each_slot(scal, place)


def halves(*shape):
    return jax.ShapeDtypeStruct((*shape, TILE, TILE), jnp.bfloat16)


SMEM = pl.BlockSpec(memory_space=pltpu.SMEM)
VMEM = pl.BlockSpec(memory_space=pltpu.VMEM)
THREE = jax.ShapeDtypeStruct((3, TILE, TILE), jnp.float32)
PAIR = jax.ShapeDtypeStruct((2, 3, TILE, TILE), jnp.float32)
NINE = jax.ShapeDtypeStruct((3, 3, TILE, TILE), jnp.float32)


def call(kernel, outs, flops, *args):
    return pl.pallas_call(
        kernel,
        out_shape=outs,
        in_specs=[SMEM] + [VMEM] * (len(args) - 1),
        out_specs=[VMEM] * len(outs),
        cost_estimate=pl.CostEstimate(flops=flops, bytes_accessed=4_000_000, transcendentals=0),
    )(*args)


def device(row, col):
    return (row % SIDE) * SIDE + col % SIDE


def send(value, pairs):
    return lax.ppermute(value, AXES, [(device(*s), device(*t)) for s, t in pairs])


class Tree:
    def __init__(self, value, roots, me):
        self.value, self.have, self.me, self.came, self.moves = (value, list(roots), me, [], ())

    def start(self, moves):
        self.moves = moves
        self.came = [send(self.value, [(s, move(*s)) for s in self.have]) for move in moves]

    def finish(self):
        mask = np.zeros(SIDE * SIDE, bool)
        for s in self.have:
            mask[device(*s)] = True
        own = jnp.asarray(mask)[self.me]
        self.value = jnp.where(own, self.value, functools.reduce(jnp.add, self.came))
        self.have += [move(*s) for move in self.moves for s in self.have]

    def after(self, other):
        self.value, _ = lax.optimization_barrier((self.value, other))


def flip_row(bits):
    return lambda row, col: (row ^ bits, col)


def turn_row(step):
    return lambda row, col: ((row + step) % SIDE, col)


def turn_col(step):
    return lambda row, col: (row, (col + step) % SIDE)


def turn_low(step):
    return lambda row, col: (row, (col & ~3) | ((col + step) & 3))


ROW_LEVELS = ((flip_row(2),), (turn_row(4), turn_row(8), turn_row(12)), (flip_row(1),))
COL_LEVELS = ((turn_col(4), turn_col(8), turn_col(12)), (turn_low(1), turn_low(2), turn_low(3)))


def program(
    rhs_c, rhs_f, pencil_a, pencil_d, pencil_b, pencil_e, d_inverse, left_vectors, left_inverse,
    left_eigs, e_inverse, right_vectors, right_inverse, right_eigs,
):
    row = lax.axis_index("row").astype(jnp.int32)
    col = lax.axis_index("col").astype(jnp.int32)
    me = row * SIDE + col
    cc, ff, pa, pd, pb, pe = [
        v.transpose(0, 2, 1, 3) for v in (rhs_c, rhs_f, pencil_a, pencil_d, pencil_b, pencil_e)
    ]
    ahead = (col - row) % SIDE
    role = jnp.where(ahead == SIDE - 1, 0, jnp.where(ahead < 2, ahead + 1, 3))
    shift = jnp.where((role == 0) & (col == SIDE - 1), 1, jnp.where((role == 2) & (col == 0), -1, 0))
    scal = jnp.stack([role, shift, row, col])
    ring = range(SIDE)
    left = (d_inverse, left_vectors, left_inverse, left_eigs)

    near_ad, near_be, a_own, e_own = call(
        near_kernel, [halves(2, 3), halves(2, 3), halves(3), halves(3)], 1_000_000, scal, pa, pd, pb, pe
    )
    col_m = send(near_ad, [((r, r + k), (r, r + k - 1)) for r in ring for k in range(3)])
    row_p = send(near_be, [((r, r + k), (r + 1, r + k)) for r in ring for k in range(3)])
    col_p = send(a_own, [((r, r), (r, r + 1)) for r in ring])
    row_m = send(e_own, [((r, r), (r - 1, r)) for r in ring])

    upper_ad, upper_be = call(
        upper_kernel, [halves(2, 6), halves(2, 6)], 20_000_000, scal, pa, pd, pb, pe
    )
    up = [(i, (i + 1) % SIDE) for i in ring]
    down = [(j, i) for i, j in up]

    ux, g, ve, du, r0, l0 = call(
        first_kernel, [THREE] * 6, 400_000_000,
        scal, cc, ff, a_own, e_own, col_m, col_p, row_p, row_m, *left,
        e_inverse, right_vectors, right_inverse, right_eigs,
    )
    ready = (*left, right_inverse, right_eigs, ux, g, ve, du)
    upper_ad, upper_be, r0, l0 = lax.optimization_barrier((upper_ad, upper_be, r0, l0))
    r0_one = send(r0, [((c + 1, c), (c, c)) for c in ring])
    l0_one = send(l0, [((r, r - 1), (r, r)) for r in ring])
    be_prev = lax.ppermute(upper_be, "row", up)
    be_next = lax.ppermute(upper_be, "row", down)
    ad_next = lax.ppermute(upper_ad, "col", down)
    ad_prev = lax.ppermute(upper_ad, "col", up)
    tiles = (scal, cc, ff, pa, pd, pb, pe, col_m, row_p)
    r1, l1 = call(
        functools.partial(next_kernel, 1), [PAIR] * 2, 400_000_000,
        *tiles, r0_one, l0_one, *ready,
    )
    r_old = send(r1, [((c, c), (c - 1, c)) for c in ring])
    l_old = send(l1, [((r, r), (r, r + 1)) for r in ring])
    r2, l2 = call(
        functools.partial(next_kernel, 2), [THREE] * 2, 400_000_000,
        *tiles, r_old, l_old, *ready,
    )

    early_r = Tree(r1, [(c, c) for c in ring], me)
    early_l = Tree(l1, [(r, r) for r in ring], me)
    late_r = Tree(r2, [((c - 1) % SIDE, c) for c in ring], me)
    late_l = Tree(l2, [(r, (r + 1) % SIDE) for r in ring], me)
    early_r.start(ROW_LEVELS[0])
    early_l.start(COL_LEVELS[0])
    late_r.start(ROW_LEVELS[0])
    late_l.start(COL_LEVELS[0])
    early_r.finish()
    early_l.finish()
    early_r.after(r2)
    early_l.after(r2)
    early_r.start(ROW_LEVELS[1])
    early_l.start(COL_LEVELS[1])
    late_r.finish()
    late_l.finish()
    late_r.start(ROW_LEVELS[1])
    late_l.start(COL_LEVELS[1])
    early_r.finish()
    early_l.finish()
    early_r.start(ROW_LEVELS[2])
    late_r.finish()
    late_l.finish()
    late_r.start(ROW_LEVELS[2])
    early_r.finish()
    late_r.finish()

    outs = call(
        last_kernel, [NINE] * 4, 1_500_000_000,
        scal, cc, ff, pa, pd, pb, pe, ad_next, ad_prev, be_prev, be_next,
        early_r.value, early_l.value, late_r.value, late_l.value, r0, l0, r1, l1, r2, l2,
    )
    return tuple(v.transpose(0, 2, 1, 3) for v in outs)


def solution(mesh):
    tile = P(None, "row", None, "col")
    lines = (P(None, "row", None),) * 3 + (P(None, "row"),)
    cols = (P(None, "col", None),) * 3 + (P(None, "col"),)
    return jax.shard_map(
        program, mesh=mesh, in_specs=(tile,) * 6 + lines + cols, out_specs=(tile,) * 4, check_vma=False
    )
```

time: 339 us -> 145 us (0.43)
  the two profiles are of different devices: /device:TPU:1 before, /device:TPU:96 now
where the time goes in v1:
time: 145 us; the launch traced here: 144 us
  waiting for transfers between devices  55.4 us (38%)
  starting transfers between devices  48.7 us (34%)
  Pallas kernels  19.4 us (13%)
  other arithmetic  10.4 us (7%)
  local copies, waits for them, and re-layouts  9.09 us (6%)
    ppermute x30, waiting for transfers between devices, send(): lax.ppermute(value, AXES, [(device(*s), device(*t)) for s, t in pairs])  39.7 us
    ppermute x30, starting transfers between devices, send(): lax.ppermute(value, AXES, [(device(*s), device(*t)) for s, t in pairs])  32.8 us
    pallas_call x6, Pallas kernels, call(): pl.pallas_call(kernel, out_shape=outs, in_specs=[SMEM] + [VMEM] * (len(ar...  19.4 us
    ppermute x1, waiting for transfers between devices, program(): be_prev = lax.ppermute(upper_be, 'row', up)  15.7 us
    ppermute x1, starting transfers between devices, program(): be_next = lax.ppermute(upper_be, 'row', down)  11.7 us
    select_n x10, other arithmetic, finish(): jnp.where(own, self.value, functools.reduce(jnp.add, self.came))  9.79 us
    dynamic_slice x8, local copies, waits for them, and re-layouts, finish(): own = jnp.asarray(mask)[self.me]  4.99 us
    ppermute x1, starting transfers between devices, program(): ad_next = lax.ppermute(upper_ad, 'col', down)  4.12 us
  transfers between devices with their start and end apart: 34, of which 4 were waited for; matrix products, arithmetic and copies ran while one was open for 10% of the time, Pallas kernels for 4%

profile of v1, /device:TPU:96, one launch (start us, length us, event | category | flops | bytes accessed | tf_op | source)
XLA Modules:
  0.0 144.4 jit_solution(4759002031344022034)
XLA Ops:
  0.7 0.6 pad_add_fusion.scal
  1.3 2.1 %shard_map.256 = (bf16[2,3,128,128]{3,2,1,0:T(8,128)(2,1)}, bf16[2,3,128,128]{3,2,1,0:T(8,128)(2,1)}, bf16[3,128,128]{2,1,0:T(8,128)(2,1)}, bf16[3,128,128]{2,1,0:T(8,128)(2,1)}) custom-call(s32[4]{0:T(128)} %pad_add_fusion.scal, bf16[3,3,128,128]{3,2,1,0:T(8,128)(2,1)} %bitcast.30, bf16[3,3,128,128]{3,2,1,0:T(8,128)(2,1)} %bitcast.35, ...), custom_call_target="tpu_custom_call" | custom-call | flops 1000000 | bytes 4000000 | tf_op jit(solution)/shard_map/pallas_call | solution.py:213
  3.3 0.7 collective-permute-start
  4.0 0.7 collective-permute-start.2
  4.7 0.7 collective-permute-start.1
  5.4 0.7 collective-permute-start.3
  6.0 2.2 %shard_map.255 = (bf16[2,6,128,128]{3,2,1,0:T(8,128)(2,1)}, bf16[2,6,128,128]{3,2,1,0:T(8,128)(2,1)}) custom-call(s32[4]{0:T(128)} %pad_add_fusion.scal, bf16[3,3,128,128]{3,2,1,0:T(8,128)(2,1)} %bitcast.31, bf16[3,3,128,128]{3,2,1,0:T(8,128)(2,1)} %bitcast.36, bf16[3,3,128,128]{3,2,1,0:T(8,128)(2,1)} %bitcast.41, bf16[3,3,128,128]{3,2,1,0:T(8,128)(2,1)} %bitcast.46), custom_call_target="tpu_custom_call" | custom-call | flops 20000000 | bytes 4000000 | tf_op jit(solution)/shard_map/pallas_call | solution.py:213
  9.0 2.9 %shard_map.257 = (f32[3,128,128]{2,1,0:T(8,128)}, f32[3,128,128]{2,1,0:T(8,128)}, f32[3,128,128]{2,1,0:T(8,128)}, f32[3,128,128]{2,1,0:T(8,128)}, f32[3,128,128]{2,1,0:T(8,128)}, /*index=5*/f32[3,128,128]{2,1,0:T(8,128)}) custom-call(s32[4]{0:T(128)} %pad_add_fusion.scal, f32[3,3,128,128]{3,2,1,0:T(8,128)} %bitcast.22, f32[3,3,128,128]{3,2,1,0:T(8,128)} %bitcast.26, ...), custom_call_target="tpu_custom_call" | custom-call | flops 400000000 | bytes 4000000 | tf_op jit(solution)/shard_map/pallas_call | solution.py:213
  11.9 0.7 collective-permute-start.8
  12.6 0.7 collective-permute-start.9
  13.3 0.6 copy-done.12
  14.1 3.3 %shard_map.258 = (f32[2,3,128,128]{3,2,1,0:T(8,128)}, f32[2,3,128,128]{3,2,1,0:T(8,128)}) custom-call(s32[4]{0:T(128)} %pad_add_fusion.scal, f32[3,3,128,128]{3,2,1,0:T(8,128)} %bitcast.23, f32[3,3,128,128]{3,2,1,0:T(8,128)} %bitcast.27, bf16[3,3,128,128]{3,2,1,0:T(8,128)(2,1)} %bitcast.32, bf16[3,3,128,128]{3,2,1,0:T(8,128)(2,1)} %bitcast.37, ...), custom_call_target="tpu_custom_call" | custom-call | flops 400000000 | bytes 4000000 | tf_op jit(solution)/shard_map/pallas_call | solution.py:213
  17.4 0.7 collective-permute-start.11
  18.0 0.7 collective-permute-start.12
  18.7 0.7 collective-permute-start.10
  19.4 1.3 collective-permute-start.19
  20.7 0.7 collective-permute-start.18
  21.4 0.7 collective-permute-start.17
  22.2 0.6 copy-done.25
  22.8 0.7 dynamic_slice.35
  23.5 0.6 dynamic_slice.30
  24.1 0.6 dynamic_slice.38
  24.8 0.6 dynamic_slice.36
  25.4 0.6 dynamic_slice.33
  26.1 0.7 dynamic_slice.31
  26.8 0.7 dynamic_slice.37
  28.0 0.7 copy-done.7
  28.8 3.2 %shard_map.259 = (f32[3,128,128]{2,1,0:T(8,128)}, f32[3,128,128]{2,1,0:T(8,128)}) custom-call(s32[4]{0:T(128)} %pad_add_fusion.scal, f32[3,3,128,128]{3,2,1,0:T(8,128)} %bitcast.24, f32[3,3,128,128]{3,2,1,0:T(8,128)} %bitcast.28, bf16[3,3,128,128]{3,2,1,0:T(8,128)(2,1)} %bitcast.33, bf16[3,3,128,128]{3,2,1,0:T(8,128)(2,1)} %bitcast.38, ...), custom_call_target="tpu_custom_call" | custom-call | flops 400000000 | bytes 4000000 | tf_op jit(solution)/shard_map/pallas_call | solution.py:213
  32.0 0.7 collective-permute-start.23
  32.7 0.7 broadcast_select_fusion
  33.6 0.7 collective-permute-start.30
  34.3 33.4 %collective-permute-done.19 = f32[2,3,128,128]{3,2,1,0:T(8,128)S(1)} collective-permute-done((f32[2,3,128,128]{3,2,1,0:T(8,128)}, f32[2,3,128,128]{3,2,1,0:T(8,128)S(1)}, u32[]{:S(2)}, u32[]{:S(2)}) %collective-permute-start.19) | collective-permute-done | bytes 393248 | tf_op jit(solution)/shard_map/ppermute | solution.py:227
  67.7 0.7 collective-permute-start.29
  68.3 0.7 collective-permute-start.28
  69.0 0.7 collective-permute-start.15
  69.7 0.6 add_select_fusion.1
  70.4 0.7 collective-permute-start.14
  71.1 1.3 collective-permute-start.13
  72.4 1.3 collective-permute-start.22
  73.7 0.8 add_select_fusion.4
  74.5 1.4 %collective-permute-start.21 = (f32[2,3,128,128]{3,2,1,0:T(8,128)S(1)}, f32[2,3,128,128]{3,2,1,0:T(8,128)S(1)}, u32[]{:S(2)}, u32[]{:S(2)}) collective-permute-start(f32[2,3,128,128]{3,2,1,0:T(8,128)S(1)} %add_select_fusion.1), channel_id=1, source_target_pairs={{0,2},{17,19},{34,32},{51,49},{68,70},{85,87},{102,100},{119,117},... | collective-permute-start | bytes 1179656 | tf_op jit(solution)/shard_map/ppermute | solution.py:227
  76.0 7.0 %collective-permute-start.20 = (f32[2,3,128,128]{3,2,1,0:T(8,128)S(1)}, f32[2,3,128,128]{3,2,1,0:T(8,128)S(1)}, u32[]{:S(2)}, u32[]{:S(2)}) collective-permute-start(f32[2,3,128,128]{3,2,1,0:T(8,128)S(1)} %add_select_fusion.1), channel_id=1, source_target_pairs={{0,1},{17,18},{34,35},{51,48},{68,69},{85,86},{102,103},{119,116},... | collective-permute-start | bytes 1179656 | tf_op jit(solution)/shard_map/ppermute | solution.py:227
  83.0 0.7 broadcast_select_fusion.2
  83.9 4.1 %collective-permute-start.4 = (bf16[2,6,128,128]{3,2,1,0:T(8,128)(2,1)S(1)}, bf16[2,6,128,128]{3,2,1,0:T(8,128)(2,1)S(1)}, u32[]{:S(2)}, u32[]{:S(2)}) collective-permute-start(bf16[2,6,128,128]{3,2,1,0:T(8,128)(2,1)S(1)} %copy-done.17), channel_id=1, source_target_pairs={{1,0},{2,1},{3,2},{4,3},{5,4},{6,5},{7,6},{8,7},{9,8},{10,9},{11,1... | collective-permute-start | bytes 1179656 | tf_op jit(solution)/shard_map/ppermute | solution.py:312
  88.0 0.7 add_select_fusion.2
  88.7 0.7 collective-permute-start.26
  89.4 0.7 collective-permute-start.25
  90.1 1.6 %collective-permute-done.20 = f32[2,3,128,128]{3,2,1,0:T(8,128)S(1)} collective-permute-done((f32[2,3,128,128]{3,2,1,0:T(8,128)S(1)}, f32[2,3,128,128]{3,2,1,0:T(8,128)S(1)}, u32[]{:S(2)}, u32[]{:S(2)}) %collective-permute-start.20) | collective-permute-done | bytes 393248 | tf_op jit(solution)/shard_map/ppermute | solution.py:227
  91.7 0.7 collective-permute-start.24
  92.4 1.5 %add_select_fusion.fl_old = f32[2,3,128,128]{3,2,1,0:T(8,128)} fusion(f32[2,3,128,128]{3,2,1,0:T(8,128)S(1)} %add_select_fusion.1, f32[2,3,128,128]{3,2,1,0:T(8,128)S(1)} %collective-permute-done.22, f32[2,3,128,128]{3,2,1,0:T(8,128)S(1)} %collective-permute-done.20, f32[2,3,128,128]{3,2,1,0:T(8,128)S(1)} %collective-permute-done.21, pred[]{:T(512)} %bitcast.13), kind=kLoop, calls=%fused_computation | loop fusion | flops 294912 | bytes 1966081 | tf_op jit(solution)/shard_map/jit(_where)/select_n | solution.py:243
  93.8 1.3 collective-permute-start.33
  95.1 0.7 collective-permute-start.32
  95.8 0.7 collective-permute-start.31
  96.5 0.7 add_select_fusion.5
  97.2 4.6 %collective-permute-done.33 = f32[3,128,128]{2,1,0:T(8,128)S(1)} collective-permute-done((f32[3,128,128]{2,1,0:T(8,128)S(1)}, f32[3,128,128]{2,1,0:T(8,128)S(1)}, u32[]{:S(2)}, u32[]{:S(2)}) %collective-permute-start.33) | collective-permute-done | bytes 196640 | tf_op jit(solution)/shard_map/ppermute | solution.py:227
  101.8 11.7 %collective-permute-start.7 = (bf16[2,6,128,128]{3,2,1,0:T(8,128)(2,1)S(1)}, bf16[2,6,128,128]{3,2,1,0:T(8,128)(2,1)S(1)}, u32[]{:S(2)}, u32[]{:S(2)}) collective-permute-start(bf16[2,6,128,128]{3,2,1,0:T(8,128)(2,1)S(1)} %copy-done.16), channel_id=1, source_target_pairs={{16,0},{32,16},{48,32},{64,48},{80,64},{96,80},{112,96},{128,112},... | collective-permute-start | bytes 1179656 | tf_op jit(solution)/shard_map/ppermute | solution.py:311
  113.6 1.3 collective-permute-start.27
  114.9 3.1 %collective-permute-start.16 = (f32[2,3,128,128]{3,2,1,0:T(8,128)S(1)}, f32[2,3,128,128]{3,2,1,0:T(8,128)S(1)}, u32[]{:S(2)}, u32[]{:S(2)}) collective-permute-start(f32[2,3,128,128]{3,2,1,0:T(8,128)S(1)} %add_select_fusion.2), channel_id=1, source_target_pairs={{0,16},{17,1},{34,50},{51,35},{68,84},{85,69},{102,118},{119,103},... | collective-permute-start | bytes 1179656 | tf_op jit(solution)/shard_map/ppermute | solution.py:227
  118.0 1.4 add_select_fusion.3.fl
  119.3 1.4 broadcast_select_fusion.3.fr
  120.7 1.4 broadcast_select_fusion.1.fr_old
  122.1 15.7 %collective-permute-done.6.be_prev = bf16[2,6,128,128]{3,2,1,0:T(8,128)(2,1)S(1)} collective-permute-done((bf16[2,6,128,128]{3,2,1,0:T(8,128)(2,1)S(1)}, bf16[2,6,128,128]{3,2,1,0:T(8,128)(2,1)S(1)}, u32[]{:S(2)}, u32[]{:S(2)}) %collective-permute-start.6) | collective-permute-done | bytes 393248 | tf_op jit(solution)/shard_map/ppermute | solution.py:310
  137.9 0.7 copy-done.11
  138.6 5.8 %shard_map.260 = (f32[3,3,128,128]{3,2,1,0:T(8,128)}, f32[3,3,128,128]{3,2,1,0:T(8,128)}, f32[3,3,128,128]{3,2,1,0:T(8,128)}, f32[3,3,128,128]{3,2,1,0:T(8,128)}) custom-call(s32[4]{0:T(128)} %pad_add_fusion.scal, f32[3,3,128,128]{3,2,1,0:T(8,128)} %bitcast.25, f32[3,3,128,128]{3,2,1,0:T(8,128)} %bitcast.29, bf16[3,3,128,128]{3,2,1,0:T(8,128)(2,1)} %bitcast.34, ...), custom_call_target="tpu_custom_call" | custom-call | flops 1500000000 | bytes 4000000 | tf_op jit(solution)/shard_map/pallas_call | solution.py:213
  (81 shorter events, 2.1 us)
Async XLA Ops:
  3.3 4.9 %collective-permute-start = (bf16[2,3,128,128]{3,2,1,0:T(8,128)(2,1)}, bf16[2,3,128,128]{3,2,1,0:T(8,128)(2,1)S(1)}, u32[]{:S(2)}, u32[]{:S(2)}) collective-permute-start(bf16[2,3,128,128]{3,2,1,0:T(8,128)(2,1)} %get-tuple-element.34), channel_id=1, source_target_pairs={{0,15},{1,0},{2,1},{17,16},{18,17},{19,18},{34,33},{35,34},{36,35}... | collective-permute-start | bytes 589832 | tf_op jit(solution)/shard_map/ppermute | solution.py:227
  4.0 4.2 %collective-permute-start.2 = (bf16[2,3,128,128]{3,2,1,0:T(8,128)(2,1)}, bf16[2,3,128,128]{3,2,1,0:T(8,128)(2,1)S(1)}, u32[]{:S(2)}, u32[]{:S(2)}) collective-permute-start(bf16[2,3,128,128]{3,2,1,0:T(8,128)(2,1)} %get-tuple-element.35), channel_id=1, source_target_pairs={{0,16},{1,17},{2,18},{17,33},{18,34},{19,35},{34,50},{35,51},{36,5... | collective-permute-start | bytes 589832 | tf_op jit(solution)/shard_map/ppermute | solution.py:227
  4.7 3.5 %collective-permute-start.1 = (bf16[3,128,128]{2,1,0:T(8,128)(2,1)}, bf16[3,128,128]{2,1,0:T(8,128)(2,1)S(1)}, u32[]{:S(2)}, u32[]{:S(2)}) collective-permute-start(bf16[3,128,128]{2,1,0:T(8,128)(2,1)} %get-tuple-element.32.a_own), channel_id=1, source_target_pairs={{0,1},{17,18},{34,35},{51,52},{68,69},{85,86},{102,103},{119,120},... | collective-permute-start | bytes 294920 | tf_op jit(solution)/shard_map/ppermute | solution.py:227
  5.4 2.8 %collective-permute-start.3 = (bf16[3,128,128]{2,1,0:T(8,128)(2,1)}, bf16[3,128,128]{2,1,0:T(8,128)(2,1)S(1)}, u32[]{:S(2)}, u32[]{:S(2)}) collective-permute-start(bf16[3,128,128]{2,1,0:T(8,128)(2,1)} %get-tuple-element.33.e_own), channel_id=1, source_target_pairs={{0,240},{17,1},{34,18},{51,35},{68,52},{85,69},{102,86},{119,103},... | collective-permute-start | bytes 294920 | tf_op jit(solution)/shard_map/ppermute | solution.py:227
  8.2 0.6 copy-start.14
  8.2 0.7 copy-start.15
  8.2 0.7 copy-start
  8.2 0.8 copy-start.1
  11.9 1.4 collective-permute-start.8
  12.6 0.7 collective-permute-start.9
  13.3 0.7 copy-start.12
  13.3 0.7 copy-start.13
  17.4 4.1 %collective-permute-start.11 = (f32[2,3,128,128]{3,2,1,0:T(8,128)}, f32[2,3,128,128]{3,2,1,0:T(8,128)S(1)}, u32[]{:S(2)}, u32[]{:S(2)}) collective-permute-start(f32[2,3,128,128]{3,2,1,0:T(8,128)} %get-tuple-element.46.r1), channel_id=1, source_target_pairs={{0,240},{17,1},{34,18},{51,35},{68,52},{85,69},{102,86},{119,103},... | collective-permute-start | bytes 1179656 | tf_op jit(solution)/shard_map/ppermute | solution.py:227
  18.0 10.0 %collective-permute-start.12 = (f32[2,3,128,128]{3,2,1,0:T(8,128)}, f32[2,3,128,128]{3,2,1,0:T(8,128)S(1)}, u32[]{:S(2)}, u32[]{:S(2)}) collective-permute-start(f32[2,3,128,128]{3,2,1,0:T(8,128)} %get-tuple-element.47.l1), channel_id=1, source_target_pairs={{0,1},{17,18},{34,35},{51,52},{68,69},{85,86},{102,103},{119,120},... | collective-permute-start | bytes 1179656 | tf_op jit(solution)/shard_map/ppermute | solution.py:227
  18.7 13.9 %collective-permute-start.10 = (f32[2,3,128,128]{3,2,1,0:T(8,128)}, f32[2,3,128,128]{3,2,1,0:T(8,128)S(1)}, u32[]{:S(2)}, u32[]{:S(2)}) collective-permute-start(f32[2,3,128,128]{3,2,1,0:T(8,128)} %get-tuple-element.46.r1), channel_id=1, source_target_pairs={{0,32},{17,49},{34,2},{51,19},{68,100},{85,117},{102,70},{119,87},... | collective-permute-start | bytes 1179656 | tf_op jit(solution)/shard_map/ppermute | solution.py:227
  19.4 48.2 %collective-permute-start.19 = (f32[2,3,128,128]{3,2,1,0:T(8,128)}, f32[2,3,128,128]{3,2,1,0:T(8,128)S(1)}, u32[]{:S(2)}, u32[]{:S(2)}) collective-permute-start(f32[2,3,128,128]{3,2,1,0:T(8,128)} %get-tuple-element.47.l1), channel_id=1, source_target_pairs={{0,12},{17,29},{34,46},{51,63},{68,64},{85,81},{102,98},{119,115},... | collective-permute-start | bytes 1179656 | tf_op jit(solution)/shard_map/ppermute | solution.py:227
  20.7 47.6 %collective-permute-start.18 = (f32[2,3,128,128]{3,2,1,0:T(8,128)}, f32[2,3,128,128]{3,2,1,0:T(8,128)S(1)}, u32[]{:S(2)}, u32[]{:S(2)}) collective-permute-start(f32[2,3,128,128]{3,2,1,0:T(8,128)} %get-tuple-element.47.l1), channel_id=1, source_target_pairs={{0,8},{17,25},{34,42},{51,59},{68,76},{85,93},{102,110},{119,127},... | collective-permute-start | bytes 1179656 | tf_op jit(solution)/shard_map/ppermute | solution.py:227
  21.4 6.6 %copy-start.6 = (f32[2,3,128,128]{3,2,1,0:T(8,128)}, f32[2,3,128,128]{3,2,1,0:T(8,128)S(1)}, u32[]{:S(2)}) copy-start(f32[2,3,128,128]{3,2,1,0:T(8,128)S(1)} %collective-permute-done.11.r_old) | copy-start | bytes 1179652
  21.4 47.6 %collective-permute-start.17 = (f32[2,3,128,128]{3,2,1,0:T(8,128)}, f32[2,3,128,128]{3,2,1,0:T(8,128)S(1)}, u32[]{:S(2)}, u32[]{:S(2)}) collective-permute-start(f32[2,3,128,128]{3,2,1,0:T(8,128)} %get-tuple-element.47.l1), channel_id=1, source_target_pairs={{0,4},{17,21},{34,38},{51,55},{68,72},{85,89},{102,106},{119,123},... | collective-permute-start | bytes 1179656 | tf_op jit(solution)/shard_map/ppermute | solution.py:227
  22.1 0.7 copy-start.25
  22.8 0.7 copy-start.24
  23.5 0.7 copy-start.23
  24.1 0.7 copy-start.22
  24.8 0.7 copy-start.21
  25.4 0.7 copy-start.20
  26.1 0.7 copy-start.19
  26.7 0.7 copy-start.18
  28.0 4.7 %copy-start.2 = (f32[2,3,128,128]{3,2,1,0:T(8,128)S(1)}, f32[2,3,128,128]{3,2,1,0:T(8,128)}, u32[]{:S(2)}) copy-start(f32[2,3,128,128]{3,2,1,0:T(8,128)} %get-tuple-element.46.r1) | copy-start | bytes 1179652
  28.0 0.7 copy-start.7
  32.0 42.6 %collective-permute-start.23 = (f32[3,128,128]{2,1,0:T(8,128)}, f32[3,128,128]{2,1,0:T(8,128)S(1)}, u32[]{:S(2)}, u32[]{:S(2)}) collective-permute-start(f32[3,128,128]{2,1,0:T(8,128)} %get-tuple-element.48.r2), channel_id=1, source_target_pairs={{240,208},{1,33},{18,50},{35,3},{52,20},{69,101},{86,118},{103,71}... | collective-permute-start | bytes 589832 | tf_op jit(solution)/shard_map/ppermute | solution.py:227
  32.7 0.9 copy-start.4
  32.7 37.0 %copy-start.3 = (f32[2,3,128,128]{3,2,1,0:T(8,128)S(1)}, f32[2,3,128,128]{3,2,1,0:T(8,128)}, u32[]{:S(2)}) copy-start(f32[2,3,128,128]{3,2,1,0:T(8,128)} %get-tuple-element.47.l1) | copy-start | bytes 1179652
  33.6 36.8 %collective-permute-start.30 = (f32[3,128,128]{2,1,0:T(8,128)S(1)}, f32[3,128,128]{2,1,0:T(8,128)S(1)}, u32[]{:S(2)}, u32[]{:S(2)}) collective-permute-start(f32[3,128,128]{2,1,0:T(8,128)S(1)} %copy-done.4), channel_id=1, source_target_pairs={{1,13},{18,30},{35,47},{52,48},{69,65},{86,82},{103,99},{120,116},... | collective-permute-start | bytes 589832 | tf_op jit(solution)/shard_map/ppermute | solution.py:227
  67.7 3.4 %collective-permute-start.29 = (f32[3,128,128]{2,1,0:T(8,128)S(1)}, f32[3,128,128]{2,1,0:T(8,128)S(1)}, u32[]{:S(2)}, u32[]{:S(2)}) collective-permute-start(f32[3,128,128]{2,1,0:T(8,128)S(1)} %copy-done.4), channel_id=1, source_target_pairs={{1,9},{18,26},{35,43},{52,60},{69,77},{86,94},{103,111},{120,112},... | collective-permute-start | bytes 589832 | tf_op jit(solution)/shard_map/ppermute | solution.py:227
  68.3 4.1 %collective-permute-start.28 = (f32[3,128,128]{2,1,0:T(8,128)S(1)}, f32[3,128,128]{2,1,0:T(8,128)S(1)}, u32[]{:S(2)}, u32[]{:S(2)}) collective-permute-start(f32[3,128,128]{2,1,0:T(8,128)S(1)} %copy-done.4), channel_id=1, source_target_pairs={{1,5},{18,22},{35,39},{52,56},{69,73},{86,90},{103,107},{120,124},... | collective-permute-start | bytes 589832 | tf_op jit(solution)/shard_map/ppermute | solution.py:227
  69.0 7.0 %collective-permute-start.15 = (f32[2,3,128,128]{3,2,1,0:T(8,128)S(1)}, f32[2,3,128,128]{3,2,1,0:T(8,128)S(1)}, u32[]{:S(2)}, u32[]{:S(2)}) collective-permute-start(f32[2,3,128,128]{3,2,1,0:T(8,128)S(1)} %broadcast_select_fusion), channel_id=1, source_target_pairs={{0,192},{17,209},{34,226},{51,243},{68,4},{85,21},{102,38},{119,55... | collective-permute-start | bytes 1179656 | tf_op jit(solution)/shard_map/ppermute | solution.py:227
  70.4 13.3 %collective-permute-start.14 = (f32[2,3,128,128]{3,2,1,0:T(8,128)S(1)}, f32[2,3,128,128]{3,2,1,0:T(8,128)S(1)}, u32[]{:S(2)}, u32[]{:S(2)}) collective-permute-start(f32[2,3,128,128]{3,2,1,0:T(8,128)S(1)} %broadcast_select_fusion), channel_id=1, source_target_pairs={{0,128},{17,145},{34,162},{51,179},{68,196},{85,213},{102,230},{11... | collective-permute-start | bytes 1179656 | tf_op jit(solution)/shard_map/ppermute | solution.py:227
  71.1 12.7 %collective-permute-start.13 = (f32[2,3,128,128]{3,2,1,0:T(8,128)S(1)}, f32[2,3,128,128]{3,2,1,0:T(8,128)S(1)}, u32[]{:S(2)}, u32[]{:S(2)}) collective-permute-start(f32[2,3,128,128]{3,2,1,0:T(8,128)S(1)} %broadcast_select_fusion), channel_id=1, source_target_pairs={{0,64},{17,81},{34,98},{51,115},{68,132},{85,149},{102,166},{119,1... | collective-permute-start | bytes 1179656 | tf_op jit(solution)/shard_map/ppermute | solution.py:227
  72.4 16.3 %collective-permute-start.22 = (f32[2,3,128,128]{3,2,1,0:T(8,128)S(1)}, f32[2,3,128,128]{3,2,1,0:T(8,128)S(1)}, u32[]{:S(2)}, u32[]{:S(2)}) collective-permute-start(f32[2,3,128,128]{3,2,1,0:T(8,128)S(1)} %add_select_fusion.1), channel_id=1, source_target_pairs={{0,3},{17,16},{34,33},{51,50},{68,71},{85,84},{102,101},{119,118},... | collective-permute-start | bytes 1179656 | tf_op jit(solution)/shard_map/ppermute | solution.py:227
  73.7 9.3 %copy-start.5 = (f32[3,128,128]{2,1,0:T(8,128)S(1)}, f32[3,128,128]{2,1,0:T(8,128)}, u32[]{:S(2)}) copy-start(f32[3,128,128]{2,1,0:T(8,128)} %get-tuple-element.48.r2) | copy-start | bytes 589828
  74.5 9.2 %copy-start.17 = (bf16[2,6,128,128]{3,2,1,0:T(8,128)(2,1)S(1)}, bf16[2,6,128,128]{3,2,1,0:T(8,128)(2,1)}, u32[]{:S(2)}) copy-start(bf16[2,6,128,128]{3,2,1,0:T(8,128)(2,1)} %get-tuple-element.38) | copy-start | bytes 1179652
  74.5 14.8 %collective-permute-start.21 = (f32[2,3,128,128]{3,2,1,0:T(8,128)S(1)}, f32[2,3,128,128]{3,2,1,0:T(8,128)S(1)}, u32[]{:S(2)}, u32[]{:S(2)}) collective-permute-start(f32[2,3,128,128]{3,2,1,0:T(8,128)S(1)} %add_select_fusion.1), channel_id=1, source_target_pairs={{0,2},{17,19},{34,32},{51,49},{68,70},{85,87},{102,100},{119,117},... | collective-permute-start | bytes 1179656 | tf_op jit(solution)/shard_map/ppermute | solution.py:227
  76.0 15.7 %collective-permute-start.20 = (f32[2,3,128,128]{3,2,1,0:T(8,128)S(1)}, f32[2,3,128,128]{3,2,1,0:T(8,128)S(1)}, u32[]{:S(2)}, u32[]{:S(2)}) collective-permute-start(f32[2,3,128,128]{3,2,1,0:T(8,128)S(1)} %add_select_fusion.1), channel_id=1, source_target_pairs={{0,1},{17,18},{34,35},{51,48},{68,69},{85,86},{102,103},{119,116},... | collective-permute-start | bytes 1179656 | tf_op jit(solution)/shard_map/ppermute | solution.py:227
  83.8 38.3 %collective-permute-start.5 = (bf16[2,6,128,128]{3,2,1,0:T(8,128)(2,1)S(1)}, bf16[2,6,128,128]{3,2,1,0:T(8,128)(2,1)S(1)}, u32[]{:S(2)}, u32[]{:S(2)}) collective-permute-start(bf16[2,6,128,128]{3,2,1,0:T(8,128)(2,1)S(1)} %copy-done.17), channel_id=1, source_target_pairs={{0,1},{1,2},{2,3},{3,4},{4,5},{5,6},{6,7},{7,8},{8,9},{9,10},{10,1... | collective-permute-start | bytes 1179656 | tf_op jit(solution)/shard_map/ppermute | solution.py:313
  83.9 38.2 %collective-permute-start.4 = (bf16[2,6,128,128]{3,2,1,0:T(8,128)(2,1)S(1)}, bf16[2,6,128,128]{3,2,1,0:T(8,128)(2,1)S(1)}, u32[]{:S(2)}, u32[]{:S(2)}) collective-permute-start(bf16[2,6,128,128]{3,2,1,0:T(8,128)(2,1)S(1)} %copy-done.17), channel_id=1, source_target_pairs={{1,0},{2,1},{3,2},{4,3},{5,4},{6,5},{7,6},{8,7},{9,8},{10,9},{11,1... | collective-permute-start | bytes 1179656 | tf_op jit(solution)/shard_map/ppermute | solution.py:312
  88.7 5.1 %collective-permute-start.26 = (f32[3,128,128]{2,1,0:T(8,128)S(1)}, f32[3,128,128]{2,1,0:T(8,128)S(1)}, u32[]{:S(2)}, u32[]{:S(2)}) collective-permute-start(f32[3,128,128]{2,1,0:T(8,128)S(1)} %broadcast_select_fusion.2), channel_id=1, source_target_pairs={{240,176},{1,193},{18,210},{35,227},{52,244},{69,5},{86,22},{103,3... | collective-permute-start | bytes 589832 | tf_op jit(solution)/shard_map/ppermute | solution.py:227
  89.4 5.7 %collective-permute-start.25 = (f32[3,128,128]{2,1,0:T(8,128)S(1)}, f32[3,128,128]{2,1,0:T(8,128)S(1)}, u32[]{:S(2)}, u32[]{:S(2)}) collective-permute-start(f32[3,128,128]{2,1,0:T(8,128)S(1)} %broadcast_select_fusion.2), channel_id=1, source_target_pairs={{240,112},{1,129},{18,146},{35,163},{52,180},{69,197},{86,214},{10... | collective-permute-start | bytes 589832 | tf_op jit(solution)/shard_map/ppermute | solution.py:227
  91.7 4.1 %collective-permute-start.24 = (f32[3,128,128]{2,1,0:T(8,128)S(1)}, f32[3,128,128]{2,1,0:T(8,128)S(1)}, u32[]{:S(2)}, u32[]{:S(2)}) collective-permute-start(f32[3,128,128]{2,1,0:T(8,128)S(1)} %broadcast_select_fusion.2), channel_id=1, source_target_pairs={{240,48},{1,65},{18,82},{35,99},{52,116},{69,133},{86,150},{103,16... | collective-permute-start | bytes 589832 | tf_op jit(solution)/shard_map/ppermute | solution.py:227
  93.8 8.0 %collective-permute-start.33 = (f32[3,128,128]{2,1,0:T(8,128)S(1)}, f32[3,128,128]{2,1,0:T(8,128)S(1)}, u32[]{:S(2)}, u32[]{:S(2)}) collective-permute-start(f32[3,128,128]{2,1,0:T(8,128)S(1)} %add_select_fusion.4), channel_id=1, source_target_pairs={{1,0},{18,17},{35,34},{52,55},{69,68},{86,85},{103,102},{120,123},... | collective-permute-start | bytes 589832 | tf_op jit(solution)/shard_map/ppermute | solution.py:227
  95.1 18.5 %collective-permute-start.32 = (f32[3,128,128]{2,1,0:T(8,128)S(1)}, f32[3,128,128]{2,1,0:T(8,128)S(1)}, u32[]{:S(2)}, u32[]{:S(2)}) collective-permute-start(f32[3,128,128]{2,1,0:T(8,128)S(1)} %add_select_fusion.4), channel_id=1, source_target_pairs={{1,3},{18,16},{35,33},{52,54},{69,71},{86,84},{103,101},{120,122},... | collective-permute-start | bytes 589832 | tf_op jit(solution)/shard_map/ppermute | solution.py:227
  95.8 19.1 %collective-permute-start.31 = (f32[3,128,128]{2,1,0:T(8,128)S(1)}, f32[3,128,128]{2,1,0:T(8,128)S(1)}, u32[]{:S(2)}, u32[]{:S(2)}) collective-permute-start(f32[3,128,128]{2,1,0:T(8,128)S(1)} %add_select_fusion.4), channel_id=1, source_target_pairs={{1,2},{18,19},{35,32},{52,53},{69,70},{86,87},{103,100},{120,121},... | collective-permute-start | bytes 589832 | tf_op jit(solution)/shard_map/ppermute | solution.py:227
  96.5 5.3 %copy-start.16 = (bf16[2,6,128,128]{3,2,1,0:T(8,128)(2,1)S(1)}, bf16[2,6,128,128]{3,2,1,0:T(8,128)(2,1)}, u32[]{:S(2)}) copy-start(bf16[2,6,128,128]{3,2,1,0:T(8,128)(2,1)} %get-tuple-element.39) | copy-start | bytes 1179652
  101.8 20.2 %collective-permute-start.7 = (bf16[2,6,128,128]{3,2,1,0:T(8,128)(2,1)S(1)}, bf16[2,6,128,128]{3,2,1,0:T(8,128)(2,1)S(1)}, u32[]{:S(2)}, u32[]{:S(2)}) collective-permute-start(bf16[2,6,128,128]{3,2,1,0:T(8,128)(2,1)S(1)} %copy-done.16), channel_id=1, source_target_pairs={{16,0},{32,16},{48,32},{64,48},{80,64},{96,80},{112,96},{128,112},... | collective-permute-start | bytes 1179656 | tf_op jit(solution)/shard_map/ppermute | solution.py:311
  113.6 5.7 %collective-permute-start.27 = (f32[3,128,128]{2,1,0:T(8,128)S(1)}, f32[3,128,128]{2,1,0:T(8,128)S(1)}, u32[]{:S(2)}, u32[]{:S(2)}) collective-permute-start(f32[3,128,128]{2,1,0:T(8,128)S(1)} %add_select_fusion.5), channel_id=1, source_target_pairs={{240,224},{1,17},{18,2},{35,51},{52,36},{69,85},{86,70},{103,119},... | collective-permute-start | bytes 589832 | tf_op jit(solution)/shard_map/ppermute | solution.py:227
  114.9 5.8 %collective-permute-start.16 = (f32[2,3,128,128]{3,2,1,0:T(8,128)S(1)}, f32[2,3,128,128]{3,2,1,0:T(8,128)S(1)}, u32[]{:S(2)}, u32[]{:S(2)}) collective-permute-start(f32[2,3,128,128]{3,2,1,0:T(8,128)S(1)} %add_select_fusion.2), channel_id=1, source_target_pairs={{0,16},{17,1},{34,50},{51,35},{68,84},{85,69},{102,118},{119,103},... | collective-permute-start | bytes 1179656 | tf_op jit(solution)/shard_map/ppermute | solution.py:227
  119.3 18.5 %collective-permute-start.6 = (bf16[2,6,128,128]{3,2,1,0:T(8,128)(2,1)S(1)}, bf16[2,6,128,128]{3,2,1,0:T(8,128)(2,1)S(1)}, u32[]{:S(2)}, u32[]{:S(2)}) collective-permute-start(bf16[2,6,128,128]{3,2,1,0:T(8,128)(2,1)S(1)} %copy-done.16), channel_id=1, source_target_pairs={{0,16},{16,32},{32,48},{48,64},{64,80},{80,96},{96,112},{112,128},... | collective-permute-start | bytes 1179656 | tf_op jit(solution)/shard_map/ppermute | solution.py:310
  122.1 15.8 %copy-start.8 = (bf16[2,6,128,128]{3,2,1,0:T(8,128)(2,1)}, bf16[2,6,128,128]{3,2,1,0:T(8,128)(2,1)S(1)}, u32[]{:S(2)}) copy-start(bf16[2,6,128,128]{3,2,1,0:T(8,128)(2,1)S(1)} %collective-permute-done.5.ad_prev) | copy-start | bytes 1179652
  122.1 15.8 %copy-start.9 = (bf16[2,6,128,128]{3,2,1,0:T(8,128)(2,1)}, bf16[2,6,128,128]{3,2,1,0:T(8,128)(2,1)S(1)}, u32[]{:S(2)}) copy-start(bf16[2,6,128,128]{3,2,1,0:T(8,128)(2,1)S(1)} %collective-permute-done.4.ad_next) | copy-start | bytes 1179652
  122.1 15.8 %copy-start.10 = (bf16[2,6,128,128]{3,2,1,0:T(8,128)(2,1)}, bf16[2,6,128,128]{3,2,1,0:T(8,128)(2,1)S(1)}, u32[]{:S(2)}) copy-start(bf16[2,6,128,128]{3,2,1,0:T(8,128)(2,1)S(1)} %collective-permute-done.7.be_next) | copy-start | bytes 1179652
  137.9 0.8 copy-start.11
